TPU v7x, 32 devices: a whole 2x2x4 slice. The times are simulated.
32 devices in a mesh: row: 4 (over y, x), col: 4 (over z), crop: 2 (over core).
Axes of the slice: x: 2, y: 2, z: 4, core: 2. Of those that a mesh axis runs over, the one named last changes fastest.
Arguments:
- pair_repr: bfloat16 [256, 128, 128], P(('crop', 'row'), 'col'), parts along dimension 0, may hold values from -6 to 6
- pair_mask: int32 [256, 128], P(('crop', 'row'), 'col'), parts along dimension 0, may hold values 0 or 1
- out_left_w: bfloat16 [128, 256], replicated, may hold values from -0.5 to 0.5
- out_right_w: bfloat16 [128, 256], replicated, may hold values from -0.5 to 0.5
- out_gate_w: bfloat16 [128, 128], replicated, may hold values from -0.5 to 0.5
- out_final_w: bfloat16 [128, 128], replicated, may hold values from -0.5 to 0.5
- in_left_w: bfloat16 [128, 256], replicated, may hold values from -0.5 to 0.5
- in_right_w: bfloat16 [128, 256], replicated, may hold values from -0.5 to 0.5
- in_gate_w: bfloat16 [128, 128], replicated, may hold values from -0.5 to 0.5
- in_final_w: bfloat16 [128, 128], replicated, may hold values from -0.5 to 0.5
- trans_in_w: bfloat16 [128, 1024], replicated, may hold values from -0.5 to 0.5
- trans_out_w: bfloat16 [512, 128], replicated, may hold values from -0.25 to 0.25
Outputs:
- pair_out: bfloat16 [256, 128, 128], P(('crop', 'row'), 'col'), parts along dimension 0
There are 2 independent parts, one for each index of `crop`. A program takes and returns all parts, laid end to end along the dimension named above; an argument that names none is the same for every part. Nothing has to cross between parts.
All inputs are finite; a program needn't handle non-finite values. No bound on the sum of `pair_mask` on one device may be relied on, other than what follows from the above.
Results may differ from a plain program's by a relative error of at most 0.015.
Values may be sent and summed in bfloat16 or wider, within the bound.
No kernel may reach another device: no remote copies, remote signals or barrier semaphores. Data moves between devices by JAX's collectives and lax.ppermute only.
A program may use at most 128 MiB of HBM per device.

v0:
```python
import jax
import jax.numpy as jnp
from jax import lax
from jax.sharding import PartitionSpec as P

epsilon = 1e-05


def layer_norm(values):
    average = jnp.mean(values, axis=-1, keepdims=True)
    centered = values - average
    spread = jnp.mean(centered * centered, axis=-1, keepdims=True)
    return centered * lax.rsqrt(spread + epsilon)


def gated(normed, weight, mask_vals):
    projected = jnp.dot(normed, weight, preferred_element_type=jnp.float32)
    half_width = weight.shape[1] // 2
    result = jax.nn.sigmoid(projected[..., :half_width]) * projected[..., half_width:]
    result = result * mask_vals[..., None]
    return result.astype(jnp.bfloat16)


def finish(pair_repr, normed, triangle, gate_w, final_w):
    gate_vals = jax.nn.sigmoid(jnp.dot(normed, gate_w, preferred_element_type=jnp.float32))
    tri_norm = layer_norm(triangle).astype(jnp.bfloat16)
    update = jnp.dot(tri_norm, final_w, preferred_element_type=jnp.float32)
    return (pair_repr.astype(jnp.float32) + gate_vals * update).astype(jnp.bfloat16)


def shards(
    pair_repr,
    pair_mask,
    out_left_w,
    out_right_w,
    out_gate_w,
    out_final_w,
    in_left_w,
    in_right_w,
    in_gate_w,
    in_final_w,
    trans_in_w,
    trans_out_w,
):
    mask_vals = pair_mask.astype(jnp.float32)
    normed_out = layer_norm(pair_repr.astype(jnp.float32)).astype(jnp.bfloat16)
    outbound = gated(normed_out, out_right_w, mask_vals)
    turned_right = lax.all_to_all(
        lax.all_to_all(outbound, "row", split_axis=0, concat_axis=0, tiled=True),
        "col",
        split_axis=0,
        concat_axis=1,
        tiled=True,
    )
    left_tile = gated(normed_out, out_left_w, mask_vals)
    gathered = lax.all_gather(left_tile, "col", axis=1, tiled=True)
    triangle = jnp.einsum(
        "ikh,jkh->ijh",
        gathered,
        lax.all_gather(turned_right, "row", axis=0, tiled=True),
        preferred_element_type=jnp.float32,
    )
    middle = finish(pair_repr, normed_out, triangle, out_gate_w, out_final_w)
    normed_in = layer_norm(middle.astype(jnp.float32)).astype(jnp.bfloat16)
    outbound_left = gated(normed_in, in_left_w, mask_vals)
    turned_left = lax.all_to_all(
        lax.all_to_all(outbound_left, "col", split_axis=1, concat_axis=1, tiled=True),
        "row",
        split_axis=1,
        concat_axis=0,
        tiled=True,
    )
    right_tile = gated(normed_in, in_right_w, mask_vals)
    column_panel = lax.all_gather(right_tile, "row", axis=0, tiled=True)
    triangle_in = jnp.einsum(
        "kih,kjh->ijh",
        lax.all_gather(turned_left, "col", axis=1, tiled=True),
        column_panel,
        preferred_element_type=jnp.float32,
    )
    after_in = finish(middle, normed_in, triangle_in, in_gate_w, in_final_w)
    normed_mix = layer_norm(after_in.astype(jnp.float32)).astype(jnp.bfloat16)
    projected = jnp.dot(normed_mix, trans_in_w, preferred_element_type=jnp.float32)
    half_width = trans_in_w.shape[1] // 2
    hidden = (jax.nn.silu(projected[..., :half_width]) * projected[..., half_width:]).astype(
        jnp.bfloat16
    )
    result = after_in.astype(jnp.float32) + jnp.dot(
        hidden, trans_out_w, preferred_element_type=jnp.float32
    )
    return result.astype(jnp.bfloat16)


def solution(mesh):
    in_specs = (
        P(("crop", "row"), "col", None),
        P(("crop", "row"), "col"),
        P(),
        P(),
        P(),
        P(),
        P(),
        P(),
        P(),
        P(),
        P(),
        P(),
    )
    out_specs = P(("crop", "row"), "col", None)
    return jax.shard_map(shards, mesh=mesh, in_specs=in_specs, out_specs=out_specs, check_vma=False)
```

profile of v0, /device:TPU:0, one launch (start us, length us, event | category | flops | bytes accessed | tf_op | source)
XLA Modules:
  0.0 162.0 jit_solution(13725264176336256992)
XLA Ops:
  6.5 1.2 convert_reduce_fusion
  7.8 1.3 fusion.17
  9.1 1.4 fusion.44
  10.6 1.3 fusion.46
  11.9 1.0 fusion.30
  13.0 10.7 %all_to_all.46 = bf16[32,32,128]{2,1,0:T(8,128)(2,1)S(1)} all-to-all(bf16[32,32,128]{2,1,0:T(8,128)(2,1)S(1)} %get-tuple-element.8), channel_id=1, replica_groups=mesh['row'=4,'col'=4,'crop'=2] {'row'}, dimensions={0} | all-to-all | bytes 524288 | tf_op jit(solution)/shard_map/all_to_all | solution.py:49
  23.7 21.0 %all_to_all.47 = bf16[32,32,128]{2,1,0:T(8,128)(2,1)S(1)} all-to-all(bf16[32,32,128]{2,1,0:T(8,128)(2,1)S(1)} %all_to_all.46), channel_id=1, replica_groups=mesh['row'=4,'col'=4,'crop'=2] {'col'}, dimensions={0} | all-to-all | bytes 524288 | tf_op jit(solution)/shard_map/all_to_all | solution.py:48
  44.7 0.9 copy.66
  45.7 0.7 fusion.6
  46.5 3.4 %all-gather.7.cloned.1.call-done = bf16[32,128,128]{2,1,0:T(8,128)(2,1)} async-done(((bf16[32,32,128]{2,1,0:T(8,128)(2,1)}), bf16[32,128,128]{2,1,0:T(8,128)(2,1)}) %all-gather.7.cloned.1.call-update) | async-done | bytes 1048592 | tf_op jit(solution)/shard_map/all_gather | solution.py:56
  49.9 2.7 %copy.67 = bf16[32,128,128]{1,0,2:T(8,128)(2,1)} copy(bf16[32,128,128]{2,1,0:T(8,128)(2,1)} %all-gather.7.cloned.1.call-done) | data formatting | bytes 2097152 | tf_op jit(solution)/shard_map/all_gather | solution.py:56
  52.5 24.4 %all-gather.5.cloned.1.call-done = bf16[32,128,128]{1,0,2:T(8,128)(2,1)} async-done(((bf16[8,128,128]{1,0,2:T(8,128)(2,1)}), bf16[32,128,128]{1,0,2:T(8,128)(2,1)}) %all-gather.5.cloned.1.call-update) | async-done | bytes 1048592 | tf_op jit(solution)/shard_map/all_gather | solution.py:60
  76.9 2.2 %bitcast_reduce_fusion.1 = (f32[32,32]{0,1:T(8,128)S(1)}, f32[128,32,32]{2,1,0:T(8,128)S(1)}) fusion(bf16[32,128,128]{1,0,2:T(8,128)(2,1)} %all-gather.5.cloned.1.call-done, bf16[32,128,128]{1,0,2:T(8,128)(2,1)} %copy.67), kind=kOutput, calls=%fused_computation.5 | convolution fusion | flops 33684480 | bytes 2625536 | tf_op jit(solution)/shard_map/ikh,jkh->ijh/dot_general | solution.py:57
  79.2 0.1 copy.68
  79.2 0.1 copy.69
  79.3 0.3 multiply_reduce_fusion.1
  79.6 0.1 copy.70
  79.7 0.1 copy.71
  79.8 1.3 multiply_convert_fusion.1
  81.1 2.7 %copy.72 = bf16[32,32,128]{2,1,0:T(8,128)(2,1)S(1)} copy(bf16[32,32,128]{0,1,2:T(8,128)(2,1)} %multiply_convert_fusion.1) | data formatting | bytes 524288 | tf_op jit(solution)/shard_map/convert_element_type | solution.py:26
  83.8 0.4 fusion.60
  84.1 0.4 multiply_reduce_fusion.3
  84.5 0.3 multiply_convert_fusion.3
  84.9 0.3 fusion.49
  85.2 0.3 fusion.51
  85.5 1.0 fusion.20
  86.5 0.1 copy.73
  86.7 13.1 %all_to_all.48 = bf16[32,32,128]{2,0,1:T(8,128)(2,1)S(1)} all-to-all(bf16[32,32,128]{2,0,1:T(8,128)(2,1)S(1)} %copy.73), channel_id=1, replica_groups=mesh['row'=4,'col'=4,'crop'=2] {'col'}, dimensions={1} | all-to-all | bytes 524288 | tf_op jit(solution)/shard_map/all_to_all | solution.py:67
  99.8 8.2 %all_to_all.49 = bf16[32,32,128]{2,0,1:T(8,128)(2,1)S(1)} all-to-all(bf16[32,32,128]{2,0,1:T(8,128)(2,1)S(1)} %all_to_all.48), channel_id=1, replica_groups=mesh['row'=4,'col'=4,'crop'=2] {'row'}, dimensions={1} | all-to-all | bytes 524288 | tf_op jit(solution)/shard_map/all_to_all | solution.py:66
  108.0 0.1 copy.75
  108.1 0.9 copy.76
  109.1 1.1 fusion.3
  110.2 3.4 %all-gather.9.cloned.1.call-done = bf16[128,32,128]{2,1,0:T(8,128)(2,1)} async-done(((bf16[32,32,128]{2,1,0:T(8,128)(2,1)}), bf16[128,32,128]{2,1,0:T(8,128)(2,1)}) %all-gather.9.cloned.1.call-update) | async-done | bytes 1048592 | tf_op jit(solution)/shard_map/all_gather | solution.py:74
  113.6 3.2 %copy.77 = bf16[128,32,128]{0,1,2:T(8,128)(2,1)} copy(bf16[128,32,128]{2,1,0:T(8,128)(2,1)} %all-gather.9.cloned.1.call-done) | data formatting | bytes 2097152 | tf_op jit(solution)/shard_map/all_gather | solution.py:74
  116.8 27.7 %all-gather.11.cloned.1.call-done = bf16[128,32,128]{0,1,2:T(8,128)(2,1)} async-done(((bf16[128,8,128]{0,1,2:T(8,128)(2,1)}), bf16[128,32,128]{0,1,2:T(8,128)(2,1)}) %all-gather.11.cloned.1.call-update) | async-done | bytes 1048592 | tf_op jit(solution)/shard_map/all_gather | solution.py:77
  144.5 2.2 %bitcast_reduce_fusion = (f32[32,32]{0,1:T(8,128)S(1)}, f32[128,32,32]{2,1,0:T(8,128)S(1)}) fusion(bf16[128,32,128]{0,1,2:T(8,128)(2,1)} %copy.77, bf16[128,32,128]{0,1,2:T(8,128)(2,1)} %all-gather.11.cloned.1.call-done), kind=kOutput, calls=%fused_computation.3 | convolution fusion | flops 33684480 | bytes 2625536 | tf_op jit(solution)/shard_map/kih,kjh->ijh/dot_general | solution.py:75
  146.7 0.1 copy.78
  146.8 0.1 copy.79
  146.9 0.3 multiply_reduce_fusion
  147.2 0.1 copy.80
  147.3 0.1 copy.81
  147.4 1.3 multiply_convert_fusion
  148.6 2.6 %copy.82 = bf16[32,32,128]{2,1,0:T(8,128)(2,1)S(1)} copy(bf16[32,32,128]{0,1,2:T(8,128)(2,1)} %multiply_convert_fusion) | data formatting | bytes 524288 | tf_op jit(solution)/shard_map/convert_element_type | solution.py:26
  151.3 1.4 fusion.61
  152.7 0.4 multiply_reduce_fusion.2
  153.1 0.8 fusion.39
  153.9 0.1 copy-done.7
  154.0 1.4 fusion.13
  (39 shorter events, 0.3 us)
Async XLA Ops:
  6.5 146.6 %copy-start = (bf16[128,1024]{1,0:T(8,128)(2,1)S(1)}, bf16[128,1024]{1,0:T(8,128)(2,1)}, u32[]{:S(2)}) copy-start(bf16[128,1024]{1,0:T(8,128)(2,1)} %param.22) | copy-start | bytes 786436
  6.5 4.0 %copy-start.1 = (bf16[32,32,128]{2,1,0:T(8,128)(2,1)S(1)}, bf16[32,32,128]{2,1,0:T(8,128)(2,1)}, u32[]{:S(2)}) copy-start(bf16[32,32,128]{2,1,0:T(8,128)(2,1)} %param.12) | copy-start | bytes 786436
  6.5 5.3 %copy-start.6 = (s32[32,32]{1,0:T(8,128)S(1)}, s32[32,32]{1,0:T(8,128)}, u32[]{:S(2)}) copy-start(s32[32,32]{1,0:T(8,128)} %param.13) | copy-start | bytes 12292
  6.5 43.3 %all-gather.7.cloned.1.call-start = ((), (), s32[]{:S(2)}) async-start(), calls=%async_computation.5 | async-start | bytes 1310720 | tf_op jit(solution)/shard_map/all_gather | solution.py:56
  11.9 33.8 %copy-start.8 = (bf16[128,128]{1,0:T(8,128)(2,1)S(1)}, bf16[128,128]{1,0:T(8,128)(2,1)}, u32[]{:S(2)}) copy-start(bf16[128,128]{1,0:T(8,128)(2,1)} %param.16) | copy-start | bytes 98308
  12.9 64.0 %all-gather.5.cloned.1.call-start = ((), (), s32[]{:S(2)}) async-start(), calls=%async_computation.4 | async-start | bytes 1310720 | tf_op jit(solution)/shard_map/all_gather | solution.py:60
  45.7 67.9 %all-gather.9.cloned.1.call-start = ((), (), s32[]{:S(2)}) async-start(), calls=%async_computation.6 | async-start | bytes 1310720 | tf_op jit(solution)/shard_map/all_gather | solution.py:74
  79.8 3.9 %copy-start.5 = (bf16[128,128]{1,0:T(8,128)(2,1)S(1)}, bf16[128,128]{1,0:T(8,128)(2,1)}, u32[]{:S(2)}) copy-start(bf16[128,128]{1,0:T(8,128)(2,1)} %param.17) | copy-start | bytes 98308
  81.1 3.8 %copy-start.2 = (bf16[128,256]{1,0:T(8,128)(2,1)S(1)}, bf16[128,256]{1,0:T(8,128)(2,1)}, u32[]{:S(2)}) copy-start(bf16[128,256]{1,0:T(8,128)(2,1)} %param.18) | copy-start | bytes 196612
  83.7 1.4 copy-start.3
  86.5 22.6 %copy-start.9 = (bf16[128,128]{1,0:T(8,128)(2,1)S(1)}, bf16[128,128]{1,0:T(8,128)(2,1)}, u32[]{:S(2)}) copy-start(bf16[128,128]{1,0:T(8,128)(2,1)} %param.20) | copy-start | bytes 98308
  86.5 58.0 %all-gather.11.cloned.1.call-start = ((), (), s32[]{:S(2)}) async-start(), calls=%async_computation.7 | async-start | bytes 1310720 | tf_op jit(solution)/shard_map/all_gather | solution.py:77
  147.4 3.9 %copy-start.4 = (bf16[128,128]{1,0:T(8,128)(2,1)S(1)}, bf16[128,128]{1,0:T(8,128)(2,1)}, u32[]{:S(2)}) copy-start(bf16[128,128]{1,0:T(8,128)(2,1)} %param.21) | copy-start | bytes 98308
  153.1 0.9 copy-start.7
Sparse Core Ops, SparseCore 0:
  13.1 36.7 all-gather.6
  51.7 25.2 all-gather.4
  86.6 26.9 all-gather.8
  115.0 29.4 all-gather.10
where the time goes:
time: 163 us; the launch traced here: 162 us
  waiting for transfers between devices  59 us (36%)
  blocking collectives  53.1 us (33%)
  local copies, waits for them, and re-layouts  14 us (9%)
  matrix products  13.4 us (8%)
  between operations  13.4 us (8%)
  other arithmetic  8.94 us (5%)
    all_gather x1, waiting for transfers between devices, shards(): lax.all_gather(turned_left, 'col', axis=1, tiled=True)  27.7 us
    all_gather x1, waiting for transfers between devices, shards(): lax.all_gather(turned_right, 'row', axis=0, tiled=True)  24.4 us
    all_to_all x1, blocking collectives, shards(): lax.all_to_all(lax.all_to_all(outbound, 'row', split_axis=0, concat_axis=...  21 us
    all_to_all x1, blocking collectives, shards(): lax.all_to_all(outbound_left, 'col', split_axis=1, concat_axis=1, tiled=T...  13.1 us
    all_to_all x1, blocking collectives, shards(): lax.all_to_all(outbound, 'row', split_axis=0, concat_axis=0, tiled=True)  10.7 us
    all_to_all x1, blocking collectives, shards(): lax.all_to_all(lax.all_to_all(outbound_left, 'col', split_axis=1, concat_...  8.25 us
    convert_element_type x2, local copies, waits for them, and re-layouts, finish(): tri_norm = layer_norm(triangle).astype(jnp.bfloat16)  5.27 us
    all_gather x1, waiting for transfers between devices, shards(): column_panel = lax.all_gather(right_tile, 'row', axis=0, tiled=True)  3.41 us
  transfers between devices with their start and end apart: 4, of which 4 were waited for; matrix products, arithmetic and copies ran while one was open for 6% of the time, Pallas kernels for 0%

commit v1 on v0

--- a/solution.py
+++ b/solution.py
@@ -72,12 +72,23 @@
     )
     right_tile = gated(normed_in, in_right_w, mask_vals)
     column_panel = lax.all_gather(right_tile, "row", axis=0, tiled=True)
-    triangle_in = jnp.einsum(
-        "kih,kjh->ijh",
-        lax.all_gather(turned_left, "col", axis=1, tiled=True),
-        column_panel,
-        preferred_element_type=jnp.float32,
-    )
+    ways, here, turn = (lax.axis_size("col"), lax.axis_index("col"), turned_left.shape[1])
+    earlier, later = ([], [])
+    going_up = going_down = turned_left
+    for far in range(ways // 2 + 1):
+        earlier.append(
+            jnp.einsum("kih,kjh->ijh", going_up, column_panel, preferred_element_type=jnp.float32)
+        )
+        if 0 < far < ways - ways // 2:
+            later.append(
+                jnp.einsum(
+                    "kih,kjh->ijh", going_down, column_panel, preferred_element_type=jnp.float32
+                )
+            )
+        going_up = lax.ppermute(going_up, "col", [(d, (d + 1) % ways) for d in range(ways)])
+        going_down = lax.ppermute(going_down, "col", [(d, (d - 1) % ways) for d in range(ways)])
+    line = jnp.concatenate([*earlier[::-1], *later], axis=0)
+    triangle_in = jnp.roll(line, (here - ways // 2) * earlier[0].shape[0], axis=0)
     after_in = finish(middle, normed_in, triangle_in, in_gate_w, in_final_w)
     normed_mix = layer_norm(after_in.astype(jnp.float32)).astype(jnp.bfloat16)
     projected = jnp.dot(normed_mix, trans_in_w, preferred_element_type=jnp.float32)

time: 163 us -> 150 us (0.920)
  waiting for transfers between devices: 59 us -> 32.2 us
  matrix products: 13.4 us -> 23 us
  starting transfers between devices: 0.13 us -> 4.34 us
    all_gather x1 -> x0, waiting for transfers between devices: 27.7 us -> none  [shards(): lax.all_gather(turned_left, 'col', axis=1, tiled=True)]
    dot_general x1 -> x4, matrix products: 2.2 us -> 11.5 us  [the longest x3 10.3 us: shards(): jnp.einsum('kih,kjh->ijh', going_up, column_panel, preferred_element_type...]
    ppermute x0 -> x3, waiting for transfers between devices: none -> 4.8 us  [the longest x2 4.8 us: shards(): lax.ppermute(going_up, 'col', [(d, (d + 1) % ways) for d in range(ways)])]
    ppermute x0 -> x3, starting transfers between devices: none -> 4.25 us  [the longest x1 3.76 us: shards(): lax.ppermute(going_down, 'col', [(d, (d - 1) % ways) for d in range(ways)])]
    all_gather x1, local copies, waits for them, and re-layouts: 3.2 us -> 7.25 us  [shards(): column_panel = lax.all_gather(right_tile, 'row', axis=0, tiled=True)]
    all_gather x1, waiting for transfers between devices: 3.41 us -> 0.01 us  [shards(): column_panel = lax.all_gather(right_tile, 'row', axis=0, tiled=True)]
    convert_element_type x2 -> x1, local copies, waits for them, and re-layouts: 5.27 us -> 2.65 us  [finish(): tri_norm = layer_norm(triangle).astype(jnp.bfloat16)]
  transfers between devices with their start and end apart: 4 -> 6, of which waited for: 4 -> 3; matrix products, arithmetic and copies ran while one was open for 6% -> 14% of each run, Pallas kernels for 0% -> 0%
where the time goes in v1:
time: 150 us; the launch traced here: 149 us
  blocking collectives  53.2 us (35%)
  waiting for transfers between devices  32.2 us (21%)
  matrix products  23 us (15%)
  local copies, waits for them, and re-layouts  15.3 us (10%)
  between operations  13.5 us (9%)
  other arithmetic  7.92 us (5%)
  starting transfers between devices  4.34 us (3%)
    all_gather x1, waiting for transfers between devices, shards(): lax.all_gather(turned_right, 'row', axis=0, tiled=True)  24.4 us
    all_to_all x1, blocking collectives, shards(): lax.all_to_all(lax.all_to_all(outbound, 'row', split_axis=0, concat_axis=...  21 us
    all_to_all x1, blocking collectives, shards(): lax.all_to_all(outbound_left, 'col', split_axis=1, concat_axis=1, tiled=T...  13.1 us
    all_to_all x1, blocking collectives, shards(): lax.all_to_all(outbound, 'row', split_axis=0, concat_axis=0, tiled=True)  10.7 us
    dot_general x3, matrix products, shards(): jnp.einsum('kih,kjh->ijh', going_up, column_panel, preferred_element_type...  10.3 us
    all_to_all x1, blocking collectives, shards(): lax.all_to_all(lax.all_to_all(outbound_left, 'col', split_axis=1, concat_...  8.36 us
    all_gather x1, local copies, waits for them, and re-layouts, shards(): column_panel = lax.all_gather(right_tile, 'row', axis=0, tiled=True)  7.25 us
    ppermute x2, waiting for transfers between devices, shards(): lax.ppermute(going_up, 'col', [(d, (d + 1) % ways) for d in range(ways)])  4.8 us
  transfers between devices with their start and end apart: 6, of which 3 were waited for; matrix products, arithmetic and copies ran while one was open for 14% of the time, Pallas kernels for 0%

profile of v1, /device:TPU:0, one launch (start us, length us, event | category | flops | bytes accessed | tf_op | source)
XLA Modules:
  0.0 149.4 jit_solution(8989359740015627291)
XLA Ops:
  6.5 1.2 convert_reduce_fusion
  7.8 1.3 fusion.17
  9.1 1.4 fusion.46
  10.6 1.3 fusion.48
  11.9 1.0 fusion.30
  13.0 10.7 %all_to_all.46 = bf16[32,32,128]{2,1,0:T(8,128)(2,1)S(1)} all-to-all(bf16[32,32,128]{2,1,0:T(8,128)(2,1)S(1)} %get-tuple-element.8), channel_id=1, replica_groups=mesh['row'=4,'col'=4,'crop'=2] {'row'}, dimensions={0} | all-to-all | bytes 524288 | tf_op jit(solution)/shard_map/all_to_all | solution.py:49
  23.7 21.0 %all_to_all.47 = bf16[32,32,128]{2,1,0:T(8,128)(2,1)S(1)} all-to-all(bf16[32,32,128]{2,1,0:T(8,128)(2,1)S(1)} %all_to_all.46), channel_id=1, replica_groups=mesh['row'=4,'col'=4,'crop'=2] {'col'}, dimensions={0} | all-to-all | bytes 524288 | tf_op jit(solution)/shard_map/all_to_all | solution.py:48
  44.7 0.9 copy.98
  45.7 1.3 fusion.6
  47.0 2.9 %all-gather.6.cloned.1.call-done = bf16[32,128,128]{2,1,0:T(8,128)(2,1)} async-done(((bf16[32,32,128]{2,1,0:T(8,128)(2,1)}), bf16[32,128,128]{2,1,0:T(8,128)(2,1)}) %all-gather.6.cloned.1.call-update) | async-done | bytes 1048592 | tf_op jit(solution)/shard_map/all_gather | solution.py:56
  49.9 2.7 %copy.99 = bf16[32,128,128]{1,0,2:T(8,128)(2,1)} copy(bf16[32,128,128]{2,1,0:T(8,128)(2,1)} %all-gather.6.cloned.1.call-done) | data formatting | bytes 2097152 | tf_op jit(solution)/shard_map/all_gather | solution.py:56
  52.5 24.4 %all-gather.4.cloned.1.call-done = bf16[32,128,128]{1,0,2:T(8,128)(2,1)} async-done(((bf16[8,128,128]{1,0,2:T(8,128)(2,1)}), bf16[32,128,128]{1,0,2:T(8,128)(2,1)}) %all-gather.4.cloned.1.call-update) | async-done | bytes 1048592 | tf_op jit(solution)/shard_map/all_gather | solution.py:60
  76.9 2.2 %bitcast_reduce_fusion = (f32[32,32]{0,1:T(8,128)S(1)}, f32[128,32,32]{2,1,0:T(8,128)S(1)}) fusion(bf16[32,128,128]{1,0,2:T(8,128)(2,1)} %all-gather.4.cloned.1.call-done, bf16[32,128,128]{1,0,2:T(8,128)(2,1)} %copy.99), kind=kOutput, calls=%fused_computation.3 | convolution fusion | flops 33684480 | bytes 2625536 | tf_op jit(solution)/shard_map/ikh,jkh->ijh/dot_general | solution.py:57
  79.3 0.3 multiply_reduce_fusion
  79.8 1.3 multiply_convert_fusion
  81.1 2.7 %copy.104 = bf16[32,32,128]{2,1,0:T(8,128)(2,1)S(1)} copy(bf16[32,32,128]{0,1,2:T(8,128)(2,1)} %multiply_convert_fusion) | data formatting | bytes 524288 | tf_op jit(solution)/shard_map/convert_element_type | solution.py:26
  83.8 1.4 fusion.63
  85.2 0.4 multiply_reduce_fusion.3
  85.6 0.3 multiply_convert_fusion.3
  86.0 0.3 fusion.51
  86.3 0.3 fusion.53
  86.5 1.0 fusion.20
  87.6 0.1 copy.105
  87.7 13.1 %all_to_all.48 = bf16[32,32,128]{2,0,1:T(8,128)(2,1)S(1)} all-to-all(bf16[32,32,128]{2,0,1:T(8,128)(2,1)S(1)} %copy.105), channel_id=1, replica_groups=mesh['row'=4,'col'=4,'crop'=2] {'col'}, dimensions={1} | all-to-all | bytes 524288 | tf_op jit(solution)/shard_map/all_to_all | solution.py:67
  100.8 8.4 %all_to_all.49 = bf16[32,32,128]{2,0,1:T(8,128)(2,1)S(1)} all-to-all(bf16[32,32,128]{2,0,1:T(8,128)(2,1)S(1)} %all_to_all.48), channel_id=1, replica_groups=mesh['row'=4,'col'=4,'crop'=2] {'row'}, dimensions={1} | all-to-all | bytes 524288 | tf_op jit(solution)/shard_map/all_to_all | solution.py:66
  109.1 0.1 copy.107
  109.2 0.2 copy.108
  109.5 0.2 collective-permute-start
  109.7 0.3 fusion.3
  110.0 3.8 %collective-permute-start.2 = (bf16[128,8,128]{0,1,2:T(8,128)(2,1)S(1)}, bf16[128,8,128]{0,1,2:T(8,128)(2,1)S(1)}, u32[]{:S(2)}, u32[]{:S(2)}) collective-permute-start(bf16[128,8,128]{0,1,2:T(8,128)(2,1)S(1)} %copy.108), channel_id=1, source_target_pairs={{0,6},{2,0},{4,2},{6,4},{1,7},{3,1},{5,3},{7,5},{8,14},{10,8},{12,... | collective-permute-start | bytes 786440 | tf_op jit(solution)/shard_map/ppermute | solution.py:89
  113.7 4.8 %collective-permute-done = bf16[128,8,128]{0,1,2:T(8,128)(2,1)S(1)} collective-permute-done((bf16[128,8,128]{0,1,2:T(8,128)(2,1)S(1)}, bf16[128,8,128]{0,1,2:T(8,128)(2,1)S(1)}, u32[]{:S(2)}, u32[]{:S(2)}) %collective-permute-start) | collective-permute-done | bytes 262176 | tf_op jit(solution)/shard_map/ppermute | solution.py:88
  118.5 0.3 collective-permute-start.1
  118.8 7.3 %copy.109 = bf16[128,32,128]{1,0,2:T(8,128)(2,1)} copy(bf16[128,32,128]{2,1,0:T(8,128)(2,1)} %all-gather.8.cloned.1.call-done) | data formatting | bytes 2097152 | tf_op jit(solution)/shard_map/all_gather | solution.py:74
  126.1 3.5 %convolution_bitcast_fusion.1 = f32[8,32,128]{1,0,2:T(8,128)S(1)} fusion(bf16[128,32,128]{1,0,2:T(8,128)(2,1)} %copy.109, bf16[128,8,128]{0,1,2:T(8,128)(2,1)S(1)} %copy.108), kind=kOutput, calls=%fused_computation.9 | convolution fusion | flops 8388608 | bytes 1441792 | tf_op jit(solution)/shard_map/kih,kjh->ijh/dot_general | solution.py:80
  129.6 1.2 convolution_bitcast_fusion
  130.8 0.2 copy.118
  131.0 0.2 copy.117
  131.2 3.4 %convolution_bitcast_fusion.2 = f32[8,32,128]{1,0,2:T(8,128)S(1)} fusion(bf16[128,32,128]{1,0,2:T(8,128)(2,1)} %copy.109, bf16[128,8,128]{0,1,2:T(8,128)(2,1)S(1)} %collective-permute-done), kind=kOutput, calls=%fused_computation.10 | convolution fusion | flops 8388608 | bytes 1441792 | tf_op jit(solution)/shard_map/kih,kjh->ijh/dot_general | solution.py:80
  134.6 0.2 copy.116
  134.8 3.4 %convolution_bitcast_fusion.3 = f32[8,32,128]{1,0,2:T(8,128)S(1)} fusion(bf16[128,32,128]{1,0,2:T(8,128)(2,1)} %copy.109, bf16[128,8,128]{0,1,2:T(8,128)(2,1)S(1)} %collective-permute-done.1), kind=kOutput, calls=%fused_computation.11 | convolution fusion | flops 8388608 | bytes 1441792 | tf_op jit(solution)/shard_map/kih,kjh->ijh/dot_general | solution.py:80
  138.2 0.2 copy.115
  138.6 0.2 dynamic-slice_reduce_fusion
  138.8 0.4 multiply_reduce_fusion.2
  139.2 0.8 fusion.64
  140.1 0.4 multiply_reduce_fusion.1
  140.5 0.8 fusion.39
  141.3 0.1 copy-done.8
  141.4 1.4 fusion.13
  (54 shorter events, 0.7 us)
Async XLA Ops:
  6.5 134.0 %copy-start = (bf16[128,1024]{1,0:T(8,128)(2,1)S(1)}, bf16[128,1024]{1,0:T(8,128)(2,1)}, u32[]{:S(2)}) copy-start(bf16[128,1024]{1,0:T(8,128)(2,1)} %param.22) | copy-start | bytes 786436
  6.5 4.0 %copy-start.2 = (bf16[32,32,128]{2,1,0:T(8,128)(2,1)S(1)}, bf16[32,32,128]{2,1,0:T(8,128)(2,1)}, u32[]{:S(2)}) copy-start(bf16[32,32,128]{2,1,0:T(8,128)(2,1)} %param.12) | copy-start | bytes 786436
  6.5 5.3 %copy-start.7 = (s32[32,32]{1,0:T(8,128)S(1)}, s32[32,32]{1,0:T(8,128)}, u32[]{:S(2)}) copy-start(s32[32,32]{1,0:T(8,128)} %param.13) | copy-start | bytes 12292
  6.5 43.3 %all-gather.6.cloned.1.call-start = ((), (), s32[]{:S(2)}) async-start(), calls=%async_computation.5 | async-start | bytes 1310720 | tf_op jit(solution)/shard_map/all_gather | solution.py:56
  11.9 33.8 %copy-start.9 = (bf16[128,128]{1,0:T(8,128)(2,1)S(1)}, bf16[128,128]{1,0:T(8,128)(2,1)}, u32[]{:S(2)}) copy-start(bf16[128,128]{1,0:T(8,128)(2,1)} %param.16) | copy-start | bytes 98308
  12.9 64.0 %all-gather.4.cloned.1.call-start = ((), (), s32[]{:S(2)}) async-start(), calls=%async_computation.4 | async-start | bytes 1310720 | tf_op jit(solution)/shard_map/all_gather | solution.py:60
  45.6 73.2 %all-gather.8.cloned.1.call-start = ((), (), s32[]{:S(2)}) async-start(), calls=%async_computation.6 | async-start | bytes 1310720 | tf_op jit(solution)/shard_map/all_gather | solution.py:74
  79.8 3.9 %copy-start.6 = (bf16[128,128]{1,0:T(8,128)(2,1)S(1)}, bf16[128,128]{1,0:T(8,128)(2,1)}, u32[]{:S(2)}) copy-start(bf16[128,128]{1,0:T(8,128)(2,1)} %param.17) | copy-start | bytes 98308
  81.1 4.9 %copy-start.3 = (bf16[128,256]{1,0:T(8,128)(2,1)S(1)}, bf16[128,256]{1,0:T(8,128)(2,1)}, u32[]{:S(2)}) copy-start(bf16[128,256]{1,0:T(8,128)(2,1)} %param.18) | copy-start | bytes 196612
  83.7 2.5 %copy-start.4 = (bf16[128,256]{1,0:T(8,128)(2,1)S(1)}, bf16[128,256]{1,0:T(8,128)(2,1)}, u32[]{:S(2)}) copy-start(bf16[128,256]{1,0:T(8,128)(2,1)} %param.19) | copy-start | bytes 196612
  87.6 22.1 %copy-start.10 = (bf16[128,128]{1,0:T(8,128)(2,1)S(1)}, bf16[128,128]{1,0:T(8,128)(2,1)}, u32[]{:S(2)}) copy-start(bf16[128,128]{1,0:T(8,128)(2,1)} %param.20) | copy-start | bytes 98308
  109.5 9.0 %collective-permute-start = (bf16[128,8,128]{0,1,2:T(8,128)(2,1)S(1)}, bf16[128,8,128]{0,1,2:T(8,128)(2,1)S(1)}, u32[]{:S(2)}, u32[]{:S(2)}) collective-permute-start(bf16[128,8,128]{0,1,2:T(8,128)(2,1)S(1)} %copy.108), channel_id=1, source_target_pairs={{0,2},{2,4},{4,6},{6,0},{1,3},{3,5},{5,7},{7,1},{8,10},{10,12},{12... | collective-permute-start | bytes 786440 | tf_op jit(solution)/shard_map/ppermute | solution.py:88
  110.0 19.7 %collective-permute-start.2 = (bf16[128,8,128]{0,1,2:T(8,128)(2,1)S(1)}, bf16[128,8,128]{0,1,2:T(8,128)(2,1)S(1)}, u32[]{:S(2)}, u32[]{:S(2)}) collective-permute-start(bf16[128,8,128]{0,1,2:T(8,128)(2,1)S(1)} %copy.108), channel_id=1, source_target_pairs={{0,6},{2,0},{4,2},{6,4},{1,7},{3,1},{5,3},{7,5},{8,14},{10,8},{12,... | collective-permute-start | bytes 786440 | tf_op jit(solution)/shard_map/ppermute | solution.py:89
  118.5 16.3 %collective-permute-start.1 = (bf16[128,8,128]{0,1,2:T(8,128)(2,1)S(1)}, bf16[128,8,128]{0,1,2:T(8,128)(2,1)S(1)}, u32[]{:S(2)}, u32[]{:S(2)}) collective-permute-start(bf16[128,8,128]{0,1,2:T(8,128)(2,1)S(1)} %collective-permute-done), channel_id=1, source_target_pairs={{0,2},{2,4},{4,6},{6,0},{1,3},{3,5},{5,7},{7,1},{8,10},{10,12},{12... | collective-permute-start | bytes 786440 | tf_op jit(solution)/shard_map/ppermute | solution.py:88
  126.1 3.5 %copy-start.1 = (bf16[128,32,128]{1,0,2:T(8,128)(2,1)S(1)}, bf16[128,32,128]{1,0,2:T(8,128)(2,1)}, u32[]{:S(2)}) copy-start(bf16[128,32,128]{1,0,2:T(8,128)(2,1)} %copy.109) | copy-start | bytes 3145732
  138.2 1.0 copy-start.5
  140.5 0.9 copy-start.8
Sparse Core Ops, SparseCore 0:
  13.1 36.7 all-gather.5
  51.7 25.2 all-gather.3
  87.7 26.8 all-gather.7
